TPU v7x, 32 devices: a whole 2x2x4 slice. The times are simulated.
32 devices in a mesh: gx: 8 (over y, x, core), gy: 4 (over z).
Axes of the slice: x: 2, y: 2, z: 4, core: 2. Of those that a mesh axis runs over, the one named last changes fastest.
Arguments:
- cells: int32 [3, 1048576], P(None, ('gx', 'gy')), may hold values from 0 to 255, as said below
- fractions: float32 [3, 1048576], P(None, ('gx', 'gy')), may hold values from 0 to 1
- charges: float32 [1048576], P(('gx', 'gy')), may hold values from -24 to 24
- influence: float32 [256, 256, 256], P('gx', 'gy'), may hold values from 0.05 to 24, as said below
- shells: int32 [256, 256, 256], P('gx', 'gy'), may hold values from 0 to 255
Outputs:
- potential_hat: float32 [2, 256, 256, 256], P(None, 'gx', 'gy')
- energy: float32 [], replicated
- virial: float32 [3, 3], replicated
- spectrum: float32 [256], replicated
Inputs may be any that keep to these rules, and one draw needn't show every extreme that they name: `cells`: atom a belongs to device a // 32768, devices numbered with gy fastest; its y cell lies in that device's block of 32 y planes (block index its gx index) and its z cell in its block of 64 z planes (block index its gy index). `influence`: Positive.
All inputs are finite; a program needn't handle non-finite values.
Results may differ from a plain program's by a relative error of at most 0.0029.
Values sent between devices are 32-bit elements; how exact they have to be, the bound alone decides.
A program may use at most 64 MiB of HBM per device.

v0:
```python
import functools
import math

import jax
import jax.numpy as jnp
import numpy as np
from jax import lax
from jax.experimental import pallas as pl
from jax.experimental.pallas import tpu as pltpu
from jax.sharding import PartitionSpec as P

MESH = 256
SHELLS = 256
SCREEN = 4096
HALO_Y = 4
HALO_Z = 8
CHUNK = 8
PACK = 16
NT = (((1,), (1,)), ((), ()))
NN = (((1,), (0,)), ((), ()))


def spline(frac):
    cube = frac * frac * frac
    square = frac * frac
    rest = 1.0 - frac
    return (
        rest * rest * rest / 6.0,
        (3.0 * cube - 6.0 * square + 4.0) / 6.0,
        (-3.0 * cube + 3.0 * square + 3.0 * frac + 1.0) / 6.0,
        cube / 6.0,
    )


def split(values):
    high = values.astype(jnp.bfloat16)
    low = (values - high.astype(jnp.float32)).astype(jnp.bfloat16)
    return high, low


def dot(left, right, dims):
    return lax.dot_general(left, right, dims, preferred_element_type=jnp.float32)


def dot3(left, right, dims):
    return (
        dot(left[0], right[0], dims) + dot(left[0], right[1], dims) + dot(left[1], right[0], dims)
    )


def table_pair(table):
    high = jnp.asarray(table.astype(np.float32)).astype(jnp.bfloat16)
    low = jnp.asarray(
        (table - table.astype(np.float32).astype(jnp.bfloat16).astype(np.float64)).astype(np.float32)
    ).astype(jnp.bfloat16)
    return high, low


def wave_tables():
    index = np.arange(MESH)
    angle = (index[:, None] * index[None, :] % MESH) * (2.0 * math.pi / MESH)
    factor = 1.0 / math.sqrt(MESH)
    return np.cos(angle) * factor, np.sin(angle) * factor


def wave_numbers(index):
    return jnp.where(index < MESH // 2, index, index - MESH).astype(jnp.float32)


def tiles_of(cell, weights, count, wrapped):
    low = cell & 7
    high = jnp.broadcast_to(cell >> 3, (8, cell.shape[1]))
    shift = lax.broadcasted_iota(jnp.int32, (8, cell.shape[1]), 0) - low
    first = jnp.zeros(shift.shape, jnp.float32)
    second = jnp.zeros(shift.shape, jnp.float32)
    for offset in range(4):
        first = jnp.where(shift == offset, weights[offset], first)
        if offset > 0:
            second = jnp.where(shift == offset - 8, weights[offset], second)
    result = []
    for tile in range(count):
        before = (tile - 1) % count if wrapped else tile - 1
        result.append(
            jnp.where(high == tile, first, jnp.where(high == before, second, 0.0))
        )
    return result


def spread_kernel(group, start, cells, fractions, charges, out, xs, ys, zs, table):
    rows_z = zs.shape[0]
    ext_y = out.shape[0] // rows_z

    @pl.when(pl.program_id(0) == 0)
    def _():
        out[...] = jnp.zeros_like(out)

    charge = charges[...]
    wx = [w * charge for w in spline(fractions[0:1, :])]
    tiles = tiles_of(cells[0:1, :], wx, MESH // 8, True)
    for pair in range(MESH // 16):
        xs[pair * 16 : pair * 16 + 16, :] = jnp.concatenate(
            tiles[2 * pair : 2 * pair + 2], axis=0
        ).astype(jnp.bfloat16)
    tiles = tiles_of(
        cells[1:2, :] - start[0], spline(fractions[1:2, :]), ys.shape[0] // 8, False
    )
    for tile, value in enumerate(tiles):
        ys[tile * 8 : tile * 8 + 8, :] = value
    tiles = tiles_of(cells[2:3, :] - start[1], spline(fractions[2:3, :]), rows_z // 8, False)
    for tile, value in enumerate(tiles):
        zs[tile * 8 : tile * 8 + 8, :] = value
    for block in range(ext_y // group):
        for y in range(0, group, 2):
            plane = block * group + y
            both = jnp.concatenate(
                [zs[...] * ys[plane : plane + 1, :], zs[...] * ys[plane + 1 : plane + 2, :]],
                axis=0,
            )
            table[block % 2, y * rows_z : (y + 2) * rows_z, :] = both.astype(jnp.bfloat16)
        begin = block * group * rows_z
        out[begin : begin + group * rows_z, :] += dot(table[block % 2], xs[...], NT)


def spread(cells, fractions, charges, start, plane_y, plane_z, block=1024):
    count = charges.shape[1]
    block = min(block, count)
    ext_y = plane_y + HALO_Y
    rows_z = plane_z + HALO_Z
    group = max(g for g in range(2, 13, 2) if ext_y % g == 0)
    out = pl.pallas_call(
        functools.partial(spread_kernel, group),
        grid_spec=pltpu.PrefetchScalarGridSpec(
            num_scalar_prefetch=1,
            grid=(count // block,),
            in_specs=[
                pl.BlockSpec((3, block), lambda i, s: (0, i)),
                pl.BlockSpec((3, block), lambda i, s: (0, i)),
                pl.BlockSpec((1, block), lambda i, s: (0, i)),
            ],
            out_specs=pl.BlockSpec((ext_y * rows_z, MESH), lambda i, s: (0, 0)),
            scratch_shapes=[
                pltpu.VMEM((MESH, block), jnp.bfloat16),
                pltpu.VMEM(((ext_y + 7) // 8 * 8, block), jnp.float32),
                pltpu.VMEM((rows_z, block), jnp.float32),
                pltpu.VMEM((2, group * rows_z, block), jnp.bfloat16),
            ],
        ),
        out_shape=jax.ShapeDtypeStruct((ext_y * rows_z, MESH), jnp.float32),
        compiler_params=pltpu.CompilerParams(vmem_limit_bytes=56 << 20),
        name="spread",
    )(start, cells, fractions, charges)
    return out.reshape(ext_y, rows_z, MESH)


def along_x_kernel(plane_z, mesh, halo_y, halo_z, high, low, out):
    first = jnp.where(pl.program_id(0) == 0, 1.0, 0.0)
    pair = (high[...], low[...])
    parts = out.shape[1]
    planes = []
    for y in range(HALO_Y):
        value = mesh[y, :plane_z, :] + first * halo_y[y, :plane_z, :]
        planes.append(
            jnp.concatenate([value[:HALO_Z] + halo_z[y], value[HALO_Z:]], axis=0)
        )
    result = dot3(pair, split(jnp.concatenate(planes, axis=0)), NT)
    for y in range(HALO_Y):
        lanes = slice(y * plane_z, (y + 1) * plane_z)
        both = jnp.concatenate([result[:MESH, lanes], result[MESH:, lanes]], axis=1)
        both = both.reshape(parts, MESH // parts, 2 * plane_z)
        for turn in range(out.shape[0]):
            out[turn, :, y] = both[:, turn * CHUNK : (turn + 1) * CHUNK]


def along_x(mesh, halo_y, halo_z, parts, plane_y, plane_z):
    cosine, sine = wave_tables()
    high, low = table_pair(np.concatenate([cosine, -sine], axis=0))
    turns = MESH // parts // CHUNK
    whole = lambda array: pl.BlockSpec(array.shape, lambda i: (0,) * array.ndim)
    return pl.pallas_call(
        functools.partial(along_x_kernel, plane_z),
        grid=(plane_y // HALO_Y,),
        in_specs=[
            pl.BlockSpec((HALO_Y,) + mesh.shape[1:], lambda i: (i, 0, 0)),
            whole(halo_y),
            pl.BlockSpec((HALO_Y,) + halo_z.shape[1:], lambda i: (i, 0, 0)),
            whole(high),
            whole(low),
        ],
        out_specs=pl.BlockSpec(
            (turns, parts, HALO_Y, CHUNK, 2 * plane_z), lambda i: (0, 0, i, 0, 0)
        ),
        out_shape=jax.ShapeDtypeStruct(
            (turns, parts, plane_y, CHUNK, 2 * plane_z), jnp.float32
        ),
        name="along_x",
    )(mesh, halo_y, halo_z, high, low)


def exchange_kernel(
    parts_y, parts_z, wave, high, low, out, arrived, made, own, send_x, take_x, send_z, take_z
):
    turns, plane_y, lanes = wave.shape[0], wave.shape[2] // CHUNK, wave.shape[3]
    half = lanes // 2
    me_x = lax.axis_index("gx")
    me_z = lax.axis_index("gy")

    def copy_x(turn, source, target):
        peer = source + target - me_x
        return pltpu.make_async_remote_copy(
            src_ref=wave.at[turn, target],
            dst_ref=arrived.at[turn, source],
            send_sem=send_x.at[turn, target],
            recv_sem=take_x.at[turn, source],
            device_id=(peer, me_z),
            device_id_type=pl.DeviceIdType.MESH,
        )

    def copy_z(turn, source, target):
        peer = source + target - me_z
        return pltpu.make_async_remote_copy(
            src_ref=made.at[turn, target],
            dst_ref=out.at[turn, source],
            send_sem=send_z.at[turn, target],
            recv_sem=take_z.at[turn, source],
            device_id=(me_x, peer),
            device_id_type=pl.DeviceIdType.MESH,
        )

    def own_x(turn):
        return pltpu.make_async_copy(
            wave.at[turn, me_x], arrived.at[turn, me_x], own.at[0, turn]
        )

    def own_z(turn):
        return pltpu.make_async_copy(made.at[turn, me_z], out.at[turn, me_z], own.at[1, turn])

    @pl.loop(0, turns)
    def _(turn):
        own_x(turn).start()

        @pl.loop(1, parts_y)
        def _(offset):
            copy_x(turn, me_x, lax.rem(me_x + offset, parts_y)).start()

    @pl.loop(0, turns)
    def _(turn):
        own_x(turn).wait()

        @pl.loop(1, parts_y)
        def _(offset):
            copy_x(turn, lax.rem(me_x + offset, parts_y), me_x).wait_recv()

        for first in range(0, CHUNK, 2):
            turned = []
            for k in range(first, first + 2):
                straight = jnp.concatenate(
                    [
                        arrived[turn, s, pl.ds(k, plane_y, stride=CHUNK), :]
                        for s in range(parts_y)
                    ],
                    axis=0,
                )
                crossed = jnp.concatenate([straight[:, half:], -straight[:, :half]], axis=1)
                turned.append(jnp.concatenate([straight, crossed], axis=0))
            values = split(jnp.concatenate(turned, axis=1))
            result = dot3((high[...], low[...]), values, NN)
            for k in range(2):
                value = result[:, k * lanes : (k + 1) * lanes]
                made[turn, :, first + k] = value.reshape(parts_z, MESH // parts_z, lanes)
        own_z(turn).start()

        @pl.loop(1, parts_z)
        def _(offset):
            copy_z(turn, me_z, lax.rem(me_z + offset, parts_z)).start()

    @pl.loop(0, turns)
    def _(turn):
        own_z(turn).wait()

        @pl.loop(1, parts_y)
        def _(offset):
            copy_x(turn, me_x, lax.rem(me_x + offset, parts_y)).wait_send()

        @pl.loop(1, parts_z)
        def _(offset):
            copy_z(turn, me_z, lax.rem(me_z + offset, parts_z)).wait_send()

        @pl.loop(1, parts_z)
        def _(offset):
            copy_z(turn, lax.rem(me_z + offset, parts_z), me_z).wait_recv()


def exchange(waves, parts_z):
    turns, parts_y, plane_y, chunk, lanes = waves.shape
    cosine, sine = wave_tables()
    high, low = table_pair(np.concatenate([cosine, sine], axis=1))
    flat = waves.reshape(turns, parts_y, plane_y * chunk, lanes)
    result = (turns, parts_z, chunk, MESH // parts_z, lanes)
    return pl.pallas_call(
        functools.partial(exchange_kernel, parts_y, parts_z),
        in_specs=[
            pl.BlockSpec(memory_space=pl.ANY),
            pl.BlockSpec(memory_space=pltpu.VMEM),
            pl.BlockSpec(memory_space=pltpu.VMEM),
        ],
        out_specs=pl.BlockSpec(memory_space=pl.ANY),
        out_shape=jax.ShapeDtypeStruct(result, jnp.float32),
        scratch_shapes=[
            pltpu.VMEM(flat.shape, jnp.float32),
            pltpu.VMEM(result, jnp.float32),
            pltpu.SemaphoreType.DMA((2, turns)),
            pltpu.SemaphoreType.DMA((turns, parts_y)),
            pltpu.SemaphoreType.DMA((turns, parts_y)),
            pltpu.SemaphoreType.DMA((turns, parts_z)),
            pltpu.SemaphoreType.DMA((turns, parts_z)),
        ],
        compiler_params=pltpu.CompilerParams(
            has_side_effects=True, vmem_limit_bytes=56 << 20
        ),
        name="exchange",
    )(flat, high, low)


def along_z_kernel(
    start, blocks, high, low, influence, shells, out, packed, total, bins
):
    _, parts, step, rows, lanes = blocks.shape
    first = pl.program_id(0) == 0

    @pl.when(first)
    def _():
        total[...] = jnp.zeros_like(total)
        bins[...] = jnp.zeros_like(bins)

    joined = jnp.concatenate(
        [blocks[0, r].reshape(step * rows, lanes) for r in range(parts)], axis=1
    )
    result = dot3(split(joined), (high[...], low[...]), NN)
    wave_y = wave_numbers(start[1] + lax.broadcasted_iota(jnp.int32, (rows, MESH), 0))
    wave_z = wave_numbers(lax.broadcasted_iota(jnp.int32, (rows, MESH), 1))
    plane = wave_y * wave_y + wave_z * wave_z
    labels = lax.broadcasted_iota(jnp.int32, (16, MESH), 0)
    for k in range(step):
        real = result[k * rows : (k + 1) * rows, :MESH]
        imag = result[k * rows : (k + 1) * rows, MESH:]
        number = start[0] + pl.program_id(0) * step + k
        wave_x = jnp.where(number < MESH // 2, number, number - MESH).astype(jnp.float32)
        squared = plane + wave_x * wave_x
        keep = jnp.where(squared > 0.0, 1.0, 0.0)
        weight = keep * influence[k]
        out[0, k] = weight * real
        out[1, k] = weight * imag
        power = real * real + imag * imag
        weighted = weight * power
        coef = weighted * (2.0 * (1.0 + squared * (1.0 / SCREEN)) / (squared + 1.0 - keep))
        total[0] += weighted
        total[1] += coef
        total[2] += coef * wave_x
        total[3] += coef * (wave_x * wave_x)
        shell = shells[k]
        upper = shell >> 4
        lower = shell & 15
        for group in range(rows // 16):
            left = []
            right = []
            for row in range(group * 16, group * 16 + 16):
                left.append(
                    jnp.where(upper[row : row + 1] == labels, power[row : row + 1], 0.0).astype(
                        jnp.bfloat16
                    )
                )
                right.append(
                    jnp.where(lower[row : row + 1] == labels, 1.0, 0.0).astype(jnp.bfloat16)
                )
            bins[...] += dot(jnp.concatenate(left, axis=0), jnp.concatenate(right, axis=0), NT)

    @pl.when(pl.program_id(0) == pl.num_programs(0) - 1)
    def _():
        one = total[1]
        over_x = total[2]
        parts = [
            total[0],
            total[3],
            over_x * wave_y,
            over_x * wave_z,
            one * wave_y * wave_y,
            one * wave_y * wave_z,
            one * wave_z * wave_z,
            jnp.zeros_like(one),
        ]
        values = jnp.concatenate(
            [jnp.sum(p, axis=0, keepdims=True) for p in parts * (PACK // 8)], axis=0
        )
        values = jnp.sum(values, axis=1, keepdims=True)
        row = lax.broadcasted_iota(jnp.int32, bins.shape, 0)
        lane = lax.broadcasted_iota(jnp.int32, bins.shape, 1)
        kept = jnp.where((row >> 4) == (lane >> 4), bins[...], 0.0)
        folded = jnp.sum(kept.reshape(16, 16, MESH), axis=0)
        spot = lax.broadcasted_iota(jnp.int32, (MESH, 128), 0)
        slot = lax.broadcasted_iota(jnp.int32, (MESH, 128), 1)
        select = jnp.where((spot & 15) == slot, 1.0, 0.0)
        shell_sums = lax.dot_general(
            folded,
            select,
            NN,
            precision=lax.Precision.HIGHEST,
            preferred_element_type=jnp.float32,
        )
        slot = lax.broadcasted_iota(jnp.int32, (PACK, 128), 1)
        packed[...] = jnp.where(slot < 16, shell_sums, values)


def along_z(moved, influence, shells, start, step=2):
    turns, parts, chunk, rows, lanes = moved.shape
    rows_k = turns * chunk
    inner = chunk // step
    plane_z = lanes // 2
    cosine, sine = wave_tables()
    table = np.zeros((parts, 2, plane_z, 2, MESH))
    cosine = cosine.reshape(parts, plane_z, MESH)
    sine = sine.reshape(parts, plane_z, MESH)
    table[:, 0, :, 0] = cosine
    table[:, 1, :, 0] = sine
    table[:, 0, :, 1] = -sine
    table[:, 1, :, 1] = cosine
    high, low = table_pair(table.reshape(2 * MESH, 2 * MESH))
    whole = lambda array: pl.BlockSpec(array.shape, lambda i, s: (0,) * array.ndim)
    place = lambda i, s: (i, 0, 0)
    return pl.pallas_call(
        along_z_kernel,
        grid_spec=pltpu.PrefetchScalarGridSpec(
            num_scalar_prefetch=1,
            grid=(rows_k // step,),
            in_specs=[
                pl.BlockSpec(
                    (1, parts, step, rows, lanes), lambda i, s: (i // inner, 0, i % inner, 0, 0)
                ),
                whole(high),
                whole(low),
                pl.BlockSpec((step, rows, MESH), place),
                pl.BlockSpec((step, rows, MESH), place),
            ],
            out_specs=[
                pl.BlockSpec((2, step, rows, MESH), lambda i, s: (0, i, 0, 0)),
                pl.BlockSpec((PACK, 128), lambda i, s: (0, 0)),
            ],
            scratch_shapes=[
                pltpu.VMEM((4, rows, MESH), jnp.float32),
                pltpu.VMEM((256, 256), jnp.float32),
            ],
        ),
        out_shape=[
            jax.ShapeDtypeStruct((2,) + influence.shape, jnp.float32),
            jax.ShapeDtypeStruct((PACK, 128), jnp.float32),
        ],
        compiler_params=pltpu.CompilerParams(vmem_limit_bytes=56 << 20),
        cost_estimate=pl.CostEstimate(
            flops=24 * MESH * MESH * rows_k * rows,
            bytes_accessed=24 * rows_k * rows * MESH,
            transcendentals=0,
        ),
        name="along_z",
    )(start, moved, high, low, influence, shells)


def total_kernel(parts_y, parts_z, *refs):
    locals_, (out, own, arrived, send, receive) = refs[:-5], refs[-5:]
    count = parts_y * parts_z
    me = lax.axis_index("gx") * parts_z + lax.axis_index("gy")
    value = locals_[0][...]
    for ref in locals_[1:]:
        value = value + ref[...]
    own[...] = value
    arrived[me] = value

    def copy_to(offset):
        target = lax.rem(me + offset, count)
        return pltpu.make_async_remote_copy(
            src_ref=own,
            dst_ref=arrived.at[me],
            send_sem=send.at[target],
            recv_sem=receive.at[me],
            device_id=(target // parts_z, lax.rem(target, parts_z)),
            device_id_type=pl.DeviceIdType.MESH,
        )

    def copy_from(offset):
        source = lax.rem(me + count - offset, count)
        return pltpu.make_async_remote_copy(
            src_ref=own,
            dst_ref=arrived.at[source],
            send_sem=send.at[source],
            recv_sem=receive.at[source],
            device_id=(source // parts_z, lax.rem(source, parts_z)),
            device_id_type=pl.DeviceIdType.MESH,
        )

    @pl.loop(1, count)
    def _(offset):
        copy_to(offset).start()

    @pl.loop(1, count)
    def _(offset):
        copy_from(offset).wait_recv()

    @pl.loop(1, count)
    def _(offset):
        copy_to(offset).wait_send()

    result = arrived[0]
    for device in range(1, count):
        result = result + arrived[device]
    out[...] = result


def total_over_devices(pieces, parts_y, parts_z):
    count = parts_y * parts_z
    return pl.pallas_call(
        functools.partial(total_kernel, parts_y, parts_z),
        in_specs=[pl.BlockSpec(memory_space=pltpu.VMEM)] * len(pieces),
        out_specs=pl.BlockSpec(memory_space=pltpu.VMEM),
        out_shape=jax.ShapeDtypeStruct((PACK, 128), jnp.float32),
        scratch_shapes=[
            pltpu.VMEM((PACK, 128), jnp.float32),
            pltpu.VMEM((count, PACK, 128), jnp.float32),
            pltpu.SemaphoreType.DMA((count,)),
            pltpu.SemaphoreType.DMA((count,)),
        ],
        compiler_params=pltpu.CompilerParams(has_side_effects=True),
        name="total_over_devices",
    )(*pieces)


def passed_along(block, axis, distance):
    devices = range(lax.axis_size(axis))
    route = [((i - distance) % len(devices), i) for i in devices]
    return lax.ppermute(block, axis, route)


def shards(cells, fractions, charges, influence, shells):
    parts_y = lax.axis_size("gx")
    parts_z = lax.axis_size("gy")
    plane_y = MESH // parts_y
    plane_z = MESH // parts_z
    rows_k = MESH // parts_y
    rows = MESH // parts_z
    place = jnp.stack([lax.axis_index("gx"), lax.axis_index("gy")]).astype(jnp.int32)
    start = place * jnp.array([plane_y, plane_z], jnp.int32)
    mesh = spread(cells, fractions, charges[None], start, plane_y, plane_z)
    halo_y = passed_along(mesh[plane_y:], "gx", 1)
    edge = mesh[:plane_y, plane_z:]
    edge = edge.at[:HALO_Y].add(halo_y[:, plane_z:])
    halo_z = passed_along(edge, "gy", 1)
    waves = along_x(mesh, halo_y, halo_z, parts_y, plane_y, plane_z)
    first = place * jnp.array([rows_k, rows], jnp.int32)
    moved = exchange(waves, parts_z)
    potential_hat, packed = along_z(moved, influence, shells, first)
    scale = 0.5 / MESH**3
    joined = total_over_devices([packed], parts_y, parts_z)
    values = joined[:, 16]
    energy = scale * values[0]
    picked = np.zeros((3, 3, PACK), np.float32)
    for spot, index in enumerate((1, 2, 3, 2, 4, 5, 3, 5, 6)):
        picked[spot // 3, spot % 3, index] = 1.0
    cross = jnp.sum(jnp.asarray(picked) * values, axis=2)
    virial = scale * (jnp.eye(3, dtype=jnp.float32) * values[0] - cross)
    spectrum = joined[:, :16].reshape(SHELLS) * (SHELLS / MESH**3)
    return (potential_hat, energy, virial, spectrum)


def solution(mesh):
    return jax.shard_map(
        shards,
        mesh=mesh,
        in_specs=(
            P(None, ("gx", "gy")),
            P(None, ("gx", "gy")),
            P(("gx", "gy")),
            P("gx", "gy", None),
            P("gx", "gy", None),
        ),
        out_specs=(P(None, "gx", "gy", None), P(), P(), P()),
        check_vma=False,
    )
```

profile of v0, /device:TPU:0, one launch (start us, length us, event | category | flops | bytes accessed | tf_op | source)
XLA Modules:
  0.0 238.1 jit_solution(11204540378418770507)
XLA Ops:
  0.6 1.2 add_multiply_fusion.start
  1.9 56.7 %spread.1 = f32[2592,256]{1,0:T(8,128)} custom-call(s32[2]{0:T(128)} %add_multiply_fusion.start, s32[3,32768]{1,0:T(4,128)} %cells.1, f32[3,32768]{1,0:T(4,128)} %fractions.1, f32[1,32768]{1,0:T(1,128)} %bitcast.12), custom_call_target="tpu_custom_call" | custom-call | tf_op jit(solution)/shard_map/spread/pallas_call | solution.py:130
  58.6 1.0 slice.57
  59.6 0.5 collective-permute-start
  60.1 1.0 slice.58
  61.1 6.3 %collective-permute-done.halo_y = f32[4,72,256]{2,1,0:T(8,128)S(1)} collective-permute-done((f32[4,72,256]{2,1,0:T(8,128)S(1)}, f32[4,72,256]{2,1,0:T(8,128)S(1)}, u32[]{:S(2)}, u32[]{:S(2)}) %collective-permute-start) | collective-permute-done | bytes 294944 | tf_op jit(solution)/shard_map/ppermute | solution.py:537
  67.4 0.0 copy-start
  67.4 0.8 fusion
  68.2 2.3 collective-permute-start.1
  70.5 6.7 %collective-permute-done.1.halo_z = f32[32,8,256]{2,1,0:T(8,128)S(1)} collective-permute-done((f32[32,8,256]{2,1,0:T(8,128)S(1)}, f32[32,8,256]{2,1,0:T(8,128)S(1)}, u32[]{:S(2)}, u32[]{:S(2)}) %collective-permute-start.1) | collective-permute-done | bytes 262176 | tf_op jit(solution)/shard_map/ppermute | solution.py:537
  77.2 0.0 copy-done
  77.2 0.7 copy-done.1
  77.9 8.1 %along_x.1 = f32[4,8,32,8,128]{4,3,2,1,0:T(8,128)} custom-call(f32[36,72,256]{2,1,0:T(8,128)} %bitcast.10, f32[4,72,256]{2,1,0:T(8,128)} %copy-done, f32[32,8,256]{2,1,0:T(8,128)} %copy-done.1, bf16[512,256]{1,0:T(8,128)(2,1)} %constant.68.high, bf16[512,256]{1,0:T(8,128)(2,1)} %constant.69.low), custom_call_target="tpu_custom_call" | custom-call | tf_op jit(solution)/shard_map/along_x/pallas_call | solution.py:179
  86.0 105.5 %exchange.1.blocks = f32[4,4,8,64,128]{4,3,2,1,0:T(8,128)} custom-call(f32[4,8,256,128]{3,2,1,0:T(8,128)} %bitcast.7, bf16[256,512]{1,0:T(8,128)(2,1)} %constant.70.high, bf16[256,512]{1,0:T(8,128)(2,1)} %constant.71.low), custom_call_target="tpu_custom_call" | custom-call | tf_op jit(solution)/shard_map/exchange/pallas_call | solution.py:299
  191.6 0.0 copy-start.2
  191.6 19.2 %along_z.1 = (f32[2,32,64,256]{3,2,1,0:T(8,128)}, f32[16,128]{1,0:T(8,128)}) custom-call(s32[2]{0:T(128)} %add_multiply_fusion.start, f32[4,4,8,64,128]{4,3,2,1,0:T(8,128)} %exchange.1.blocks, bf16[512,512]{1,0:T(8,128)(2,1)} %constant.72.high, bf16[512,512]{1,0:T(8,128)(2,1)} %constant.73.low, f32[32,64,256]{2,1,0:T(8,128)} %influence.1, s32[32,64,256]{2,1,0:T(8,128)} %shells.1), custom_call_target="tpu_custom_call" | custom-call | flops 3221225472 | bytes 12582912 | tf_op jit(solution)/shard_map/along_z/pallas_call | solution.py:429
  210.8 20.7 %total_over_devices.1 = f32[16,128]{1,0:T(8,128)} custom-call(f32[16,128]{1,0:T(8,128)} %get-tuple-element.19.refs_0_), custom_call_target="tpu_custom_call" | custom-call | tf_op jit(solution)/shard_map/total_over_devices/pallas_call | solution.py:518
  231.5 1.3 slice.54
  232.8 0.9 slice_reduce_fusion
  233.7 0.7 slice_multiply_fusion
  234.4 0.6 mul.48
  235.7 0.0 copy-done.2
  235.7 0.1 multiply_reduce_fusion
  235.7 1.2 subtract_multiply_fusion
  (1 shorter events, 0.0 us)
Async XLA Ops:
  59.6 7.8 %collective-permute-start = (f32[4,72,256]{2,1,0:T(8,128)S(1)}, f32[4,72,256]{2,1,0:T(8,128)S(1)}, u32[]{:S(2)}, u32[]{:S(2)}) collective-permute-start(f32[4,72,256]{2,1,0:T(8,128)S(1)} %bitcast.11), channel_id=1, source_target_pairs={{28,0},{0,4},{4,8},{8,12},{12,16},{16,20},{20,24},{24,28},{29,1},{... | collective-permute-start | bytes 884744 | tf_op jit(solution)/shard_map/ppermute | solution.py:537
  67.4 9.8 %copy-start = (f32[4,72,256]{2,1,0:T(8,128)}, f32[4,72,256]{2,1,0:T(8,128)S(1)}, u32[]{:S(2)}) copy-start(f32[4,72,256]{2,1,0:T(8,128)S(1)} %collective-permute-done.halo_y) | copy-start | bytes 884740
  68.2 9.0 %collective-permute-start.1 = (f32[32,8,256]{2,1,0:T(8,128)S(1)}, f32[32,8,256]{2,1,0:T(8,128)S(1)}, u32[]{:S(2)}, u32[]{:S(2)}) collective-permute-start(f32[32,8,256]{2,1,0:T(8,128)S(1)} %fusion), channel_id=1, source_target_pairs={{3,0},{0,1},{1,2},{2,3},{7,4},{4,5},{5,6},{6,7},{11,8},{8,9},{9,10... | collective-permute-start | bytes 786440 | tf_op jit(solution)/shard_map/ppermute | solution.py:537
  77.2 0.7 copy-start.1
  191.6 44.1 %copy-start.2 = (f32[3,3,16]{2,1,0:T(4,128)S(1)}, f32[3,3,16]{2,1,0:T(4,128)}, u32[]{:S(2)}) copy-start(f32[3,3,16]{2,1,0:T(4,128)} %constant.67.clone) | copy-start | bytes 1732
where the time goes:
time: 239 us; the launch traced here: 238 us
  Pallas kernels  210 us (88%)
  waiting for transfers between devices  13 us (5%)
  local copies, waits for them, and re-layouts  5.48 us (2%)
  other arithmetic  4.02 us (2%)
  starting transfers between devices  2.88 us (1%)
  between operations  2.45 us (1%)
    pallas_call x1, Pallas kernels, exchange(): pl.pallas_call(functools.partial(exchange_kernel, parts_y, parts_z), in_s...  106 us
    pallas_call x1, Pallas kernels, spread(): pl.pallas_call(functools.partial(spread_kernel, group), grid_spec=pltpu.P...  56.7 us
    pallas_call x1, Pallas kernels, total_over_devices(): pl.pallas_call(functools.partial(total_kernel, parts_y, parts_z), in_spec...  20.7 us
    pallas_call x1, Pallas kernels, along_z(): pl.pallas_call(along_z_kernel, grid_spec=pltpu.PrefetchScalarGridSpec(num...  19.2 us
    ppermute x2, waiting for transfers between devices, passed_along(): return lax.ppermute(block, axis, route)  13 us
    pallas_call x1, Pallas kernels, along_x(): pl.pallas_call(functools.partial(along_x_kernel, plane_z), grid=(plane_y...  8.09 us
  transfers between devices with their start and end apart: 2, of which 2 were waited for; matrix products, arithmetic and copies ran while one was open for 0% of the time, Pallas kernels for 0%

commit v1 on v0

v1 whole, which is shorter than its diff:
```python
import functools
import math

import jax
import jax.numpy as jnp
import numpy as np
from jax import lax
from jax.experimental import pallas as pl
from jax.experimental.pallas import tpu as pltpu
from jax.sharding import PartitionSpec as P

MESH = 256
SHELLS = 256
SCREEN = 4096
HALO_Y = 4
HALO_Z = 3
PLANES = 8
GROUP = 4
BLOCK = 1024
SUBS = 8
FIRST_SUBS = 4
BUFFERS = 4
PACK = 16
SIXTH = 1.0 / 6.0
AHEAD = (9, 9, 7, 1)
NT = (((1,), (1,)), ((), ()))
NN = (((1,), (0,)), ((), ()))


def spline(frac):
    cube = frac * frac * frac
    square = frac * frac
    rest = 1.0 - frac
    return (
        rest * rest * rest * SIXTH,
        (3.0 * cube - 6.0 * square + 4.0) * SIXTH,
        (-3.0 * cube + 3.0 * square + 3.0 * frac + 1.0) * SIXTH,
        cube * SIXTH,
    )


def split(values):
    high = values.astype(jnp.bfloat16)
    low = (values - high.astype(jnp.float32)).astype(jnp.bfloat16)
    return high, low


def dot(left, right, dims):
    return lax.dot_general(left, right, dims, preferred_element_type=jnp.float32)


def dot3(left, right, dims):
    return (
        dot(left[0], right[0], dims) + dot(left[0], right[1], dims) + dot(left[1], right[0], dims)
    )


def table_pair(table):
    high = jnp.asarray(table.astype(np.float32)).astype(jnp.bfloat16)
    low = jnp.asarray(
        (table - table.astype(np.float32).astype(jnp.bfloat16).astype(np.float64)).astype(np.float32)
    ).astype(jnp.bfloat16)
    return high, low


def wave_tables():
    index = np.arange(MESH)
    angle = (index[:, None] * index[None, :] % MESH) * (2.0 * math.pi / MESH)
    factor = 1.0 / math.sqrt(MESH)
    return np.cos(angle) * factor, np.sin(angle) * factor


def wave_numbers(index):
    return jnp.where(index < MESH // 2, index, index - MESH).astype(jnp.float32)


def tiles_of(cell, weights, rows, kind):
    shape = (rows, cell.shape[1])
    row = lax.broadcasted_iota(jnp.int32, shape, 0)
    low = cell & (rows - 1)
    shift = (row - low) & (rows - 1)
    value = jnp.zeros(shape, jnp.float32)
    for offset in range(4):
        value = jnp.where(shift == offset, weights[offset], value)
    tile = (cell // rows) + jnp.where(row < low, 1, 0)
    return value.astype(kind), tile


def tables():
    cosine, sine = wave_tables()
    along_x = np.concatenate([cosine, -sine], axis=0)
    return cosine, sine, along_x


def table_y(cosine, sine, parts_z):
    rows = MESH // parts_z
    table = np.zeros((2, MESH, parts_z, max(2 * rows, 128)))
    cosine = cosine.reshape(MESH, parts_z, rows)
    sine = sine.reshape(MESH, parts_z, rows)
    table[0, :, :, :rows] = cosine
    table[0, :, :, rows : 2 * rows] = -sine
    table[1, :, :, :rows] = sine
    table[1, :, :, rows : 2 * rows] = cosine
    return table.reshape(2 * MESH, -1)


def whole_kernel(
    parts_y, parts_z,
    cells, fractions, charges, influence, shells, tx_hbm, wy_hbm, wz_hbm,
    out, joined,
    xs_all, xst_all, ys_all, zw_all, zc_all, xst, ys, zw, zc, table, acc, halo_y, edge, halo_z, wave, arrived, made, landed,
    tx, wy, wz, weights, labels_in, total, bins, pack_own, pack_z, pack_sum, pack_x, staged,
    load, send_hy, take_hy, send_hz, take_hz, send_x, take_x, send_z, take_z, store,
    send_rz, take_rz, send_rx, take_rx,
):
    ny = MESH // parts_y
    nz = MESH // parts_z
    nkx = MESH // parts_y
    nky = MESH // parts_z
    ext_y = ny + HALO_Y
    chunks = nz // PLANES
    turns = nkx // GROUP
    ahead = [AHEAD[4 * t // turns] for t in range(turns)]
    atoms = charges.shape[1]
    me_x = lax.axis_index("gx")
    me_z = lax.axis_index("gy")
    mesh_id = pl.DeviceIdType.MESH

    loads = [
        pltpu.make_async_copy(tx_hbm, tx, load.at[0]),
        pltpu.make_async_copy(wy_hbm, wy, load.at[1]),
        pltpu.make_async_copy(wz_hbm, wz, load.at[2]),
        pltpu.make_async_copy(influence, weights, load.at[3]),
        pltpu.make_async_copy(shells, labels_in, load.at[4]),
    ]
    for item in loads:
        item.start()

    barrier = pltpu.get_barrier_semaphore()

    @pl.loop(1, parts_y)
    def _(offset):
        pl.semaphore_signal(
            barrier, inc=1, device_id=(lax.rem(me_x + offset, parts_y), me_z), device_id_type=mesh_id
        )

    @pl.loop(1, parts_z)
    def _(offset):
        pl.semaphore_signal(
            barrier, inc=1, device_id=(me_x, lax.rem(me_z + offset, parts_z)), device_id_type=mesh_id
        )

    def remote(source, target, send, receive, device):
        return pltpu.make_async_remote_copy(
            src_ref=source,
            dst_ref=target,
            send_sem=send,
            recv_sem=receive,
            device_id=device,
            device_id_type=mesh_id,
        )

    next_x = lax.rem(me_x + 1, parts_y)
    next_z = lax.rem(me_z + 1, parts_z)

    def copy_hy(turn):
        return remote(
            acc.at[turn, :, pl.ds(ny * PLANES, HALO_Y * PLANES)],
            halo_y.at[turn],
            send_hy,
            take_hy.at[turn],
            (next_x, me_z),
        )

    def copy_hz():
        return remote(edge, halo_z, send_hz, take_hz, (me_x, next_z))

    def copy_x(chunk, source, target):
        return remote(
            wave.at[chunk, target],
            arrived.at[chunk, source],
            send_x,
            take_x.at[chunk],
            (source + target - me_x, me_z),
        )

    def copy_z(chunk, part, source, target):
        return remote(
            made.at[chunk, target, part],
            landed.at[chunk, source, part],
            send_z,
            take_z.at[part],
            (me_x, source + target - me_z),
        )

    start_y = me_x * ny
    start_z = me_z * nz

    def prepare(block, lanes):
        xs, xst_own, ys_own, zw_own, zc_own = (
            xs_all.at[block],
            xst_all.at[block],
            ys_all.at[block],
            zw_all.at[block],
            zc_all.at[block],
        )
        splines = spline(fractions[:, lanes])
        charge = charges[0:1, lanes]
        value, place = tiles_of(
            cells[0:1, lanes], [w[0:1] * charge for w in splines], 16, jnp.bfloat16
        )
        place = (place & (MESH // 16 - 1)).astype(jnp.float32).astype(jnp.bfloat16)
        none = jnp.zeros_like(value)
        for tile in range(MESH // 16):
            xs[tile * 16 : tile * 16 + 16, :] = jnp.where(
                place == jnp.bfloat16(tile), value, none
            )
        turned = xs[...].T
        xst_own[...] = turned
        xst[lanes, :] = turned
        value, place = tiles_of(
            cells[1:2, lanes] - start_y, [w[1:2] for w in splines], 8, jnp.float32
        )
        for tile in range(ys.shape[0] // 8):
            rows = jnp.where(place == tile, value, 0.0)
            ys_own[tile * 8 : tile * 8 + 8, :] = rows
            ys[tile * 8 : tile * 8 + 8, lanes] = rows
        for offset in range(4):
            zw_own[offset : offset + 1, :] = splines[offset][2:3]
            zw[offset : offset + 1, lanes] = splines[offset][2:3]
        spot = cells[2:3, lanes] - start_z
        zc_own[...] = spot
        zc[0:1, lanes] = spot
        return (xst_own, ys_own, zw_own, zc_own), slice(0, BLOCK)


    halo_turn = min(4, chunks - 1)

    def chunk_of(turn):
        later = jnp.where(turn == halo_turn, chunks, jnp.where(turn == chunks, 0, turn))
        return jnp.where(turn < halo_turn, turn + 1, later)

    steps = atoms // (BLOCK * SUBS)

    def spread_block(refs, lanes, base, buffer):
        xst, ys, zw, zc = refs
        shift = lax.broadcasted_iota(jnp.int32, (8, BLOCK), 0) - (zc[0:1, lanes] - base)
        zt = jnp.zeros((8, BLOCK), jnp.float32)
        for offset in range(4):
            zt = jnp.where(shift == offset, zw[offset : offset + 1, lanes], zt)
        for y in range(0, ext_y, 2):
            both = jnp.concatenate(
                [zt * ys[y : y + 1, lanes], zt * ys[y + 1 : y + 2, lanes]], axis=0
            )
            buffer[y * 8 : (y + 2) * 8, :] = both.astype(jnp.bfloat16)
        return dot(buffer[...], xst[lanes, :], NN)

    def spread_steps(turn, first, last, subs, fresh):
        base = chunk_of(turn) * PLANES

        @pl.loop(first, last)
        def _(block):
            sums = None
            for sub in range(subs):
                lanes = pl.ds(pl.multiple_of((block * subs + sub) * BLOCK, BLOCK), BLOCK)
                refs = (xst, ys, zw, zc)
                if fresh:
                    refs, lanes = prepare(sub, lanes)
                part = spread_block(refs, lanes, base, table.at[sub % BUFFERS])
                sums = part if sums is None else sums + part
            for half in range(2):
                acc[turn, half] += sums[:, half * 128 : (half + 1) * 128]

    def clear(turn):
        acc[turn] = jnp.zeros(acc.shape[1:], jnp.float32)

    @jax.named_scope("spread")
    def spread(turn, first, last):
        spread_steps(turn, first, last, SUBS, False)

    with jax.named_scope("first"):
        clear(0)
        spread_steps(0, 0, atoms // (BLOCK * FIRST_SUBS), FIRST_SUBS, True)
    with jax.named_scope("wait_barrier"):
        pl.semaphore_wait(barrier, parts_y + parts_z - 2)
        for item in loads:
            item.wait()
    copy_hy(0).start()

    @jax.named_scope("stage_x")
    def stage_x(turn):
        with jax.named_scope("wait_hy"):
            copy_hy(turn).wait_recv()
        acc[turn, :, 0 : HALO_Y * PLANES, :] += halo_y[turn]

        @pl.when(turn == halo_turn)
        def _():
            for z in range(HALO_Z):
                for half in range(2):
                    edge[half, z * ny : (z + 1) * ny, :] = acc[
                        turn, half, pl.ds(z, ny, stride=PLANES), :
                    ]
            copy_hz().start()

        @pl.when(turn == chunks)
        def _():
            copy_hz().wait_recv()
            for z in range(HALO_Z):
                for half in range(2):
                    acc[turn, half, pl.ds(z, ny, stride=PLANES), :] += halo_z[
                        half, z * ny : (z + 1) * ny, :
                    ]

        @pl.when(turn != halo_turn)
        def _():
            chunk = chunk_of(turn)
            values = jnp.concatenate(
                [
                    jnp.concatenate(
                        [acc[turn, half, pl.ds(z, ny, stride=PLANES), :] for half in range(2)],
                        axis=1,
                    )
                    for z in range(PLANES)
                ],
                axis=0,
            )
            result = dot3((tx[0], tx[1]), split(values), NT)
            lanes = PLANES * ny
            wave[chunk, :, 0:nkx, :] = result[:MESH].reshape(parts_y, nkx, lanes)
            wave[chunk, :, nkx : 2 * nkx, :] = result[MESH:].reshape(parts_y, nkx, lanes)

            @pl.loop(1, parts_y)
            def _(offset):
                copy_x(chunk, me_x, lax.rem(me_x + offset, parts_y)).start()

            arrived[chunk, me_x] = wave[chunk, me_x]

    def send_part(chunk, part):
        half = parts_z // 2
        mine, spot = me_z // half, me_z % half

        @pl.loop(0, half)
        def _(offset):
            copy_z(chunk, part, me_z, (1 - mine) * half + (spot + offset) % half).start()

        @pl.loop(1, half)
        def _(offset):
            copy_z(chunk, part, me_z, mine * half + (spot + offset) % half).start()

    @jax.named_scope("wait_x")
    def wait_x(chunk):
        span = arrived.at[chunk, pl.ds(0, parts_y - 1)]
        pltpu.make_async_copy(span, span, take_x.at[chunk]).wait()

    @jax.named_scope("stage_y")
    def stage_y(turn):
        chunk = chunk_of(turn)
        wait_x(chunk)

        rows = []
        for z in range(PLANES):
            lanes = slice(z * ny, (z + 1) * ny)
            both = [
                arrived[chunk, s, part * nkx : (part + 1) * nkx, lanes]
                for part in range(2)
                for s in range(parts_y)
            ]
            rows.append(jnp.concatenate(both, axis=1))
        values = split(jnp.concatenate(rows, axis=0))
        result = dot3(values, (wy[0], wy[1]), NN)
        width = made.shape[4]
        for q in range(parts_z):
            lanes = slice(q * width, (q + 1) * width)
            for t in range(turns):
                for z in range(PLANES):
                    row = z * nkx + t * GROUP
                    made[chunk, q, t, z * GROUP : (z + 1) * GROUP, :] = result[
                        row : row + GROUP, lanes
                    ]
        for t in range(turns):

            @pl.when(turn < ahead[t])
            def _():
                send_part(chunk, t)

        landed[chunk, me_z] = made[chunk, me_z]

    @pl.loop(1, chunks + 3)
    def _(turn):
        @pl.when(turn <= chunks)
        def _():
            clear(turn)
            spread(turn, 0, steps // 2)

        @pl.when(turn <= chunks + 1)
        def _():
            stage_x(turn - 1)

        @pl.when(jnp.logical_and(turn >= 2, turn != halo_turn + 2))
        def _():
            stage_y(turn - 2)

        @pl.when(turn <= chunks)
        def _():
            spread(turn, steps // 2, steps)
            copy_hy(turn).start()

    for t in range(turns):

        @pl.loop(min(ahead[t], chunks + 1), chunks + 1)
        def _(turn):
            @pl.when(turn != halo_turn)
            def _():
                send_part(chunk_of(turn), t)

    total[...] = jnp.zeros_like(total)
    bins[...] = jnp.zeros_like(bins)
    wave_y = wave_numbers(me_z * nky + lax.broadcasted_iota(jnp.int32, (nky, MESH), 0))
    wave_z = wave_numbers(lax.broadcasted_iota(jnp.int32, (nky, MESH), 1))

    @jax.named_scope("wait_z")
    def take_part(part):
        span = landed.at[:, pl.ds(0, parts_z - 1), 0]
        pltpu.make_async_copy(span, span, take_z.at[part]).wait()

    @jax.named_scope("final")
    def final(t):
        plane = wave_y * wave_y + wave_z * wave_z
        labels = lax.broadcasted_iota(jnp.int32, (16, MESH), 0)

        @pl.loop(0, GROUP // 2)
        def _(pair):
            turned = []
            for k in range(2):
                cube = jnp.concatenate(
                    [
                        landed[chunk, q, t, pl.ds(pair * 2 + k, PLANES, stride=GROUP), :]
                        for q in range(parts_z)
                        for chunk in range(chunks)
                    ],
                    axis=0,
                )
                turned.append(cube.T[: 2 * nky])
            result = dot3(split(jnp.concatenate(turned, axis=0)), (wz[0], wz[1]), NN)
            for k in range(2):
                first = result[2 * k * nky : (2 * k + 1) * nky]
                second = result[(2 * k + 1) * nky : (2 * k + 2) * nky]
                real = first[:, :MESH] + second[:, MESH:]
                imag = second[:, :MESH] - first[:, MESH:]
                index = t * GROUP + pair * 2 + k
                number = me_x * nkx + index
                wave_x = jnp.where(number < MESH // 2, number, number - MESH).astype(jnp.float32)
                squared = plane + wave_x * wave_x
                keep = jnp.where(squared > 0.0, 1.0, 0.0)
                weight = keep * weights[index]
                staged[0, index] = weight * real
                staged[1, index] = weight * imag
                power = real * real + imag * imag
                weighted = weight * power
                coef = weighted * (
                    2.0 * (1.0 + squared * (1.0 / SCREEN)) / (squared + 1.0 - keep)
                )
                total[0] += weighted
                total[1] += coef
                total[2] += coef * wave_x
                total[3] += coef * (wave_x * wave_x)
                shell = labels_in[index]
                upper = shell >> 4
                lower = shell & 15
                sums = None
                for group in range(nky // 16):
                    left = []
                    right = []
                    for row in range(group * 16, group * 16 + 16):
                        left.append(
                            jnp.where(
                                upper[row : row + 1] == labels, power[row : row + 1], 0.0
                            ).astype(jnp.bfloat16)
                        )
                        right.append(
                            jnp.where(lower[row : row + 1] == labels, 1.0, 0.0).astype(
                                jnp.bfloat16
                            )
                        )
                    part = dot(
                        jnp.concatenate(left, axis=0), jnp.concatenate(right, axis=0), NT
                    )
                    sums = part if sums is None else sums + part
                bins[...] += sums

    @pl.loop(0, turns)
    def _(t):
        take_part(t)
        final(t)
        rows = pl.ds(t * GROUP, GROUP)
        pltpu.make_async_copy(staged.at[:, rows], out.at[:, rows], store).start()

    one = total[1]
    over_x = total[2]
    parts = [
        total[0],
        total[3],
        over_x * wave_y,
        over_x * wave_z,
        one * wave_y * wave_y,
        one * wave_y * wave_z,
        one * wave_z * wave_z,
        jnp.zeros_like(one),
    ]
    values = jnp.concatenate(
        [jnp.sum(p, axis=0, keepdims=True) for p in parts], axis=0
    )
    values = jnp.sum(values, axis=1, keepdims=True)
    row = lax.broadcasted_iota(jnp.int32, bins.shape, 0)
    lane = lax.broadcasted_iota(jnp.int32, bins.shape, 1)
    kept = jnp.where((row >> 4) == (lane >> 4), bins[...], 0.0)
    folded = jnp.sum(kept.reshape(16, 16, MESH), axis=0)
    select = jnp.where((row & 15) == (lane & 15), 1.0, 0.0)
    shell_sums = lax.dot_general(
        folded,
        select,
        NN,
        precision=lax.Precision.HIGHEST,
        preferred_element_type=jnp.float32,
    )
    shell_sums = jnp.where(row[:16] == (lane[:16] >> 4), shell_sums, 0.0)
    shell_sums = jnp.sum(shell_sums, axis=0, keepdims=True)
    slot = lax.broadcasted_iota(jnp.int32, (8, 128), 0)
    sums = jnp.where(slot == 0, shell_sums[:, :128], shell_sums[:, 128:])
    mine = jnp.concatenate([jnp.broadcast_to(values, (8, 128)), sums], axis=0)

    def copy_rz(source, target):
        return remote(
            pack_own, pack_z.at[source], send_rz, take_rz,
            (me_x, source + target - me_z),
        )

    def copy_rx(source, target):
        return remote(
            pack_sum, pack_x.at[source], send_rx, take_rx,
            (source + target - me_x, me_z),
        )

    pack_own[...] = mine
    pack_z[me_z] = mine

    @pl.loop(1, parts_z)
    def _(offset):
        copy_rz(me_z, lax.rem(me_z + offset, parts_z)).start()

    def wait_all(group, count, semaphore):
        span = group.at[pl.ds(0, count)]
        pltpu.make_async_copy(span, span, semaphore).wait()

    with jax.named_scope("wait_rz"):
        wait_all(pack_z, parts_z - 1, take_rz)

    value = pack_z[0]
    for q in range(1, parts_z):
        value = value + pack_z[q]
    pack_sum[...] = value
    pack_x[me_x] = value

    @pl.loop(1, parts_y)
    def _(offset):
        copy_rx(me_x, lax.rem(me_x + offset, parts_y)).start()

    pltpu.make_async_copy(staged, out, store).wait()
    span = halo_y.at[:]
    pltpu.make_async_copy(span, span, send_hy).wait()
    copy_hz().wait_send()
    span = wave.at[:, pl.ds(0, parts_y - 1)]
    pltpu.make_async_copy(span, span, send_x).wait()
    span = made.at[:, pl.ds(0, parts_z - 1)]
    pltpu.make_async_copy(span, span, send_z).wait()

    with jax.named_scope("wait_rx"):
        wait_all(pack_x, parts_y - 1, take_rx)

    value = pack_x[0]
    for p in range(1, parts_y):
        value = value + pack_x[p]
    joined[...] = value

    wait_all(pack_z, parts_z - 1, send_rz)
    wait_all(pack_x, parts_y - 1, send_rx)


def whole(cells, fractions, charges, influence, shells, parts_y, parts_z):
    atoms = charges.shape[1]
    ny = MESH // parts_y
    nz = MESH // parts_z
    nkx = MESH // parts_y
    nky = MESH // parts_z
    ext_y = ny + HALO_Y
    chunks = nz // PLANES
    turns = nkx // GROUP
    cosine, sine, along_x = tables()
    tx = jnp.stack(table_pair(along_x))
    wy = jnp.stack(table_pair(table_y(cosine, sine, parts_z)))
    wz = jnp.stack(table_pair(np.concatenate([cosine, sine], axis=1)))
    f32, bf16 = jnp.float32, jnp.bfloat16
    vmem = pltpu.VMEM
    dma = lambda *shape: pltpu.SemaphoreType.DMA(shape)
    return pl.pallas_call(
        functools.partial(whole_kernel, parts_y, parts_z),
        in_specs=[pl.BlockSpec(memory_space=pltpu.VMEM)] * 3
        + [pl.BlockSpec(memory_space=pl.ANY)] * 5,
        out_specs=[
            pl.BlockSpec(memory_space=pl.ANY),
            pl.BlockSpec(memory_space=pltpu.VMEM),
        ],
        out_shape=[
            jax.ShapeDtypeStruct((2,) + influence.shape, f32),
            jax.ShapeDtypeStruct((PACK, 128), f32),
        ],
        scratch_shapes=[
            vmem((FIRST_SUBS, MESH, BLOCK), bf16),
            vmem((FIRST_SUBS, BLOCK, MESH), bf16),
            vmem((FIRST_SUBS, (ext_y + 7) // 8 * 8, BLOCK), f32),
            vmem((FIRST_SUBS, 4, BLOCK), f32),
            vmem((FIRST_SUBS, 1, BLOCK), jnp.int32),
            vmem((atoms, MESH), bf16),
            vmem(((ext_y + 7) // 8 * 8, atoms), f32),
            vmem((4, atoms), f32),
            vmem((1, atoms), jnp.int32),
            vmem((BUFFERS, ext_y * PLANES, BLOCK), bf16),
            vmem((chunks + 1, 2, ext_y * PLANES, MESH // 2), f32),
            vmem((chunks + 1, 2, HALO_Y * PLANES, MESH // 2), f32),
            vmem((2, HALO_Z * ny, MESH // 2), f32),
            vmem((2, HALO_Z * ny, MESH // 2), f32),
            vmem((chunks, parts_y, 2 * nkx, PLANES * ny), f32),
            vmem((chunks, parts_y, 2 * nkx, PLANES * ny), f32),
            vmem((chunks, parts_z, turns, PLANES * GROUP, max(2 * nky, 128)), f32),
            vmem((chunks, parts_z, turns, PLANES * GROUP, max(2 * nky, 128)), f32),
            vmem(tx.shape, bf16),
            vmem(wy.shape, bf16),
            vmem(wz.shape, bf16),
            vmem(influence.shape, f32),
            vmem(shells.shape, jnp.int32),
            vmem((4, nky, MESH), f32),
            vmem((MESH, MESH), f32),
            vmem((PACK, 128), f32),
            vmem((parts_z, PACK, 128), f32),
            vmem((PACK, 128), f32),
            vmem((parts_y, PACK, 128), f32),
            vmem((2,) + influence.shape, f32),
            dma(5),
            pltpu.SemaphoreType.DMA,
            dma(chunks + 1),
            pltpu.SemaphoreType.DMA,
            pltpu.SemaphoreType.DMA,
            pltpu.SemaphoreType.DMA,
            dma(chunks),
            pltpu.SemaphoreType.DMA,
            dma(turns),
            pltpu.SemaphoreType.DMA,
            pltpu.SemaphoreType.DMA,
            pltpu.SemaphoreType.DMA,
            pltpu.SemaphoreType.DMA,
            pltpu.SemaphoreType.DMA,
        ],
        compiler_params=pltpu.CompilerParams(
            collective_id=0, has_side_effects=True, vmem_limit_bytes=58 << 20
        ),
        name="whole",
    )(cells, fractions, charges, influence, shells, tx, wy, wz)


def finish_kernel(hat, joined, out, energy, virial, spectrum, moved, take, give):
    count = moved.shape[1]
    step = hat.shape[1] // count
    spots = [(part, index) for part in range(2) for index in range(count)]

    def copy_in(part, index):
        rows = pl.ds(index * step, step)
        return pltpu.make_async_copy(
            hat.at[part, rows], moved.at[part, index], take.at[part, index]
        )

    def copy_out(part, index):
        rows = pl.ds(index * step, step)
        return pltpu.make_async_copy(
            moved.at[part, index], out.at[part, rows], give.at[part, index]
        )

    for spot in spots:
        copy_in(*spot).start()
    scale = 0.5 / MESH**3
    values = [joined[index : index + 1, 0:1] for index in range(7)]
    energy[...] = scale * values[0]
    row = lax.broadcasted_iota(jnp.int32, (3, 3), 0)
    column = lax.broadcasted_iota(jnp.int32, (3, 3), 1)
    result = jnp.where(row == column, values[0], 0.0)
    for spot, index in enumerate((1, 2, 3, 2, 4, 5, 3, 5, 6)):
        here = jnp.logical_and(row == spot // 3, column == spot % 3)
        result = result - jnp.where(here, values[index], 0.0)
    virial[...] = scale * result
    spectrum[...] = joined[8:10, :] * (SHELLS / MESH**3)
    for spot in spots:
        copy_in(*spot).wait()
        copy_out(*spot).start()
    for spot in spots:
        copy_out(*spot).wait()


def finish(hat, joined, count=4):
    step = hat.shape[1] // count
    f32 = jnp.float32
    return pl.pallas_call(
        finish_kernel,
        in_specs=[
            pl.BlockSpec(memory_space=pl.ANY),
            pl.BlockSpec(memory_space=pltpu.VMEM),
        ],
        out_specs=[pl.BlockSpec(memory_space=pl.ANY)]
        + [pl.BlockSpec(memory_space=pltpu.VMEM)] * 3,
        out_shape=[
            jax.ShapeDtypeStruct(hat.shape, f32),
            jax.ShapeDtypeStruct((1, 1), f32),
            jax.ShapeDtypeStruct((3, 3), f32),
            jax.ShapeDtypeStruct((2, 128), f32),
        ],
        scratch_shapes=[
            pltpu.VMEM((2, count, step) + hat.shape[2:], f32),
            pltpu.SemaphoreType.DMA((2, count)),
            pltpu.SemaphoreType.DMA((2, count)),
        ],
        compiler_params=pltpu.CompilerParams(vmem_limit_bytes=62 << 20),
        name="finish",
    )(hat, joined)


def shards(cells, fractions, charges, influence, shells):
    parts_y = lax.axis_size("gx")
    parts_z = lax.axis_size("gy")
    hat, joined = whole(cells, fractions, charges[None], influence, shells, parts_y, parts_z)
    potential_hat, energy, virial, spectrum = finish(hat, joined)
    return (potential_hat, energy.reshape(()), virial, spectrum.reshape(SHELLS))


def solution(mesh):
    return jax.shard_map(
        shards,
        mesh=mesh,
        in_specs=(
            P(None, ("gx", "gy")),
            P(None, ("gx", "gy")),
            P(("gx", "gy")),
            P("gx", "gy", None),
            P("gx", "gy", None),
        ),
        out_specs=(P(None, "gx", "gy", None), P(), P(), P()),
        check_vma=False,
    )
```

time: 239 us -> 140 us (0.59)
  Pallas kernels: 210 us -> 139 us
  waiting for transfers between devices: 13 us -> 0 us
  local copies, waits for them, and re-layouts: 5.48 us -> 0 us
  other arithmetic: 4.02 us -> 0 us
  starting transfers between devices: 2.88 us -> 0 us
    pallas_call x5 -> x2, Pallas kernels: 210 us -> 139 us  [the longest x1 135 us: whole(): pl.pallas_call(functools.partial(whole_kernel, parts_y, parts_z), in_spec...]
    ppermute x2 -> x0, waiting for transfers between devices: 13 us -> none  [passed_along(): return lax.ppermute(block, axis, route)]
    slice x4 -> x0, local copies, waits for them, and re-layouts: 4.1 us -> none  [the longest x1 1.28 us: shards(): energy = scale * values[0]]
    mul x3 -> x0, other arithmetic: 3.17 us -> none  [the longest x1 1.24 us: shards(): first = place * jnp.array([rows_k, rows], jnp.int32)]
    ppermute x2 -> x0, starting transfers between devices: 2.88 us -> none  [passed_along(): return lax.ppermute(block, axis, route)]
  transfers between devices with their start and end apart: 2 -> 0, of which waited for: 2 -> 0; matrix products, arithmetic and copies ran while one was open for 0% -> 0% of each run, Pallas kernels for 0% -> 0%
where the time goes in v1:
time: 140 us
  Pallas kernels  139 us (99%)
    pallas_call x1, Pallas kernels, whole(): pl.pallas_call(functools.partial(whole_kernel, parts_y, parts_z), in_spec...  135 us
    pallas_call x1, Pallas kernels, finish(): pl.pallas_call(finish_kernel, in_specs=[pl.BlockSpec(memory_space=pl.ANY)...  4.85 us

profile of v1, /device:TPU:0, one launch (start us, length us, event | category | flops | bytes accessed | tf_op | source)
XLA Modules:
  0.0 140.1 jit_solution(15677067196096487888)
XLA Ops:
  0.6 134.6 %whole.1 = (f32[2,32,64,256]{3,2,1,0:T(8,128)}, f32[16,128]{1,0:T(8,128)}) custom-call(s32[3,32768]{1,0:T(4,128)} %cells.1, f32[3,32768]{1,0:T(4,128)} %fractions.1, f32[1,32768]{1,0:T(1,128)} %bitcast.3, f32[32,64,256]{2,1,0:T(8,128)} %influence.1, s32[32,64,256]{2,1,0:T(8,128)} %shells.1, bf16[2,512,256]{2,1,0:T(8,128)(2,1)} %constant.22.tx_hbm, ...), custom_call_target="tpu_custom_call" | custom-call | tf_op jit(solution)/shard_map/whole/pallas_call | solution.py:605
  135.2 4.9 %finish.1 = (f32[2,32,64,256]{3,2,1,0:T(8,128)}, f32[1,1]{1,0:T(1,128)}, f32[3,3]{1,0:T(4,128)}, f32[2,128]{1,0:T(2,128)}) custom-call(f32[2,32,64,256]{3,2,1,0:T(8,128)} %get-tuple-element.10.hat, f32[16,128]{1,0:T(8,128)} %get-tuple-element.11.joined), custom_call_target="tpu_custom_call" | custom-call | tf_op jit(solution)/shard_map/finish/pallas_call | solution.py:710

commit v2 on v1

--- a/solution.py
+++ b/solution.py
@@ -18,7 +18,7 @@
 GROUP = 4
 BLOCK = 1024
 SUBS = 8
-FIRST_SUBS = 4
+FIRST_SUBS = 8
 BUFFERS = 4
 PACK = 16
 SIXTH = 1.0 / 6.0
@@ -198,11 +198,11 @@
 
     def prepare(block, lanes):
         xs, xst_own, ys_own, zw_own, zc_own = (
-            xs_all.at[block],
-            xst_all.at[block],
-            ys_all.at[block],
-            zw_all.at[block],
-            zc_all.at[block],
+            xs_all.at[block % BUFFERS],
+            xst_all.at[block % BUFFERS],
+            ys_all.at[block % BUFFERS],
+            zw_all.at[block % BUFFERS],
+            zc_all.at[block % BUFFERS],
         )
         splines = spline(fractions[:, lanes])
         charge = charges[0:1, lanes]
@@ -615,11 +615,11 @@
             jax.ShapeDtypeStruct((PACK, 128), f32),
         ],
         scratch_shapes=[
-            vmem((FIRST_SUBS, MESH, BLOCK), bf16),
-            vmem((FIRST_SUBS, BLOCK, MESH), bf16),
-            vmem((FIRST_SUBS, (ext_y + 7) // 8 * 8, BLOCK), f32),
-            vmem((FIRST_SUBS, 4, BLOCK), f32),
-            vmem((FIRST_SUBS, 1, BLOCK), jnp.int32),
+            vmem((BUFFERS, MESH, BLOCK), bf16),
+            vmem((BUFFERS, BLOCK, MESH), bf16),
+            vmem((BUFFERS, (ext_y + 7) // 8 * 8, BLOCK), f32),
+            vmem((BUFFERS, 4, BLOCK), f32),
+            vmem((BUFFERS, 1, BLOCK), jnp.int32),
             vmem((atoms, MESH), bf16),
             vmem(((ext_y + 7) // 8 * 8, atoms), f32),
             vmem((4, atoms), f32),
@@ -661,7 +661,7 @@
             pltpu.SemaphoreType.DMA,
         ],
         compiler_params=pltpu.CompilerParams(
-            collective_id=0, has_side_effects=True, vmem_limit_bytes=58 << 20
+            collective_id=0, has_side_effects=True, vmem_limit_bytes=67043328
         ),
         name="whole",
     )(cells, fractions, charges, influence, shells, tx, wy, wz)

time: 140 us -> 139 us (level)
    pallas_call x1, Pallas kernels: 135 us -> 133 us  [whole(): pl.pallas_call(functools.partial(whole_kernel, parts_y, parts_z), in_spec...]
where the time goes in v2:
time: 139 us
  Pallas kernels  138 us (99%)
    pallas_call x1, Pallas kernels, whole(): pl.pallas_call(functools.partial(whole_kernel, parts_y, parts_z), in_spec...  133 us
    pallas_call x1, Pallas kernels, finish(): pl.pallas_call(finish_kernel, in_specs=[pl.BlockSpec(memory_space=pl.ANY)...  4.85 us

profile of v2, /device:TPU:0, one launch (start us, length us, event | category | flops | bytes accessed | tf_op | source)
XLA Modules:
  0.0 138.6 jit_solution(15269437480869450991)
XLA Ops:
  0.6 133.1 %whole.1 = (f32[2,32,64,256]{3,2,1,0:T(8,128)}, f32[16,128]{1,0:T(8,128)}) custom-call(s32[3,32768]{1,0:T(4,128)} %cells.1, f32[3,32768]{1,0:T(4,128)} %fractions.1, f32[1,32768]{1,0:T(1,128)} %bitcast.3, f32[32,64,256]{2,1,0:T(8,128)} %influence.1, s32[32,64,256]{2,1,0:T(8,128)} %shells.1, bf16[2,512,256]{2,1,0:T(8,128)(2,1)} %constant.22.tx_hbm, ...), custom_call_target="tpu_custom_call" | custom-call | tf_op jit(solution)/shard_map/whole/pallas_call | solution.py:605
  133.7 4.9 %finish.1 = (f32[2,32,64,256]{3,2,1,0:T(8,128)}, f32[1,1]{1,0:T(1,128)}, f32[3,3]{1,0:T(4,128)}, f32[2,128]{1,0:T(2,128)}) custom-call(f32[2,32,64,256]{3,2,1,0:T(8,128)} %get-tuple-element.10.hat, f32[16,128]{1,0:T(8,128)} %get-tuple-element.11.joined), custom_call_target="tpu_custom_call" | custom-call | tf_op jit(solution)/shard_map/finish/pallas_call | solution.py:710
